TPU v7x, 32 devices: a whole 2x2x4 slice. The times are simulated.
32 devices in a mesh: branch: 4 (over z), row: 4 (over y, x), col: 2 (over core).
Axes of the slice: x: 2, y: 2, z: 4, core: 2. Of those that a mesh axis runs over, the one named last changes fastest.
Arguments:
- section_in: bfloat16 [4, 4, 2, 48, 4096], P('branch', 'row', 'col'), may hold values from -6 to 6
- conv_weight: bfloat16 [4, 2, 3, 3, 384, 384], P('branch'), may hold values from -1 to 1, as said below
- conv_bias: float32 [4, 2, 384], P('branch'), may hold values from -3 to 3
- join_weight: bfloat16 [720, 720], replicated, may hold values from -0.4375 to 0.4375
- join_bias: float32 [720], replicated, may hold values from -3 to 3
Outputs:
- joined_first: bfloat16 [48, 128, 256], P(None, ('branch', 'row'), 'col')
- joined_second: bfloat16 [96, 64, 128], P(None, ('branch', 'row'), 'col')
- joined_third: bfloat16 [192, 32, 64], P(None, ('branch', 'row'), 'col')
- joined_fourth: bfloat16 [384, 16, 32], P(None, ('branch', 'row'), 'col')
Inputs may be any that keep to these rules, and one draw needn't show every extreme that they name: `conv_weight`: entries of branch b's kernels have standard deviation (9 * 2^b * 48) ** -0.5; entries outside the C_b x C_b corner are drawn too and unused.
All inputs are finite; a program needn't handle non-finite values.
Results may differ from a plain program's by a relative error of at most 0.0075.
Values may be sent and summed in bfloat16 or wider, within the bound.
A program may use at most 128 MiB of HBM per device.

v0:
```python
from functools import partial

import jax
import jax.numpy as jnp
from jax import lax
from jax.experimental import pallas as pl
from jax.experimental.pallas import tpu as pltpu
from jax.sharding import PartitionSpec as P

WIDTH = 48
TH = 32
TW = 128


def row_pitch(branch_level):
    return 2 * TW >> branch_level


def natural_tile(branch_level, container_ref):
    pixels = TH * TW >> 2 * branch_level
    if branch_level == 0:
        return container_ref[...].astype(jnp.float32)
    channels = WIDTH << branch_level
    parts = []
    for part in range(1 << branch_level):
        at = part * pixels
        low = at // LANES * LANES
        piece = container_ref[:, low : low + max(pixels, LANES)]
        if at > low:
            piece = pltpu.roll(piece.astype(jnp.float32), LANES - at + low, 1).astype(jnp.bfloat16)
        parts.append(piece)
    held = lax.broadcasted_iota(jnp.int32, (1, channels), 1)
    part = sum((held >= WIDTH * turn).astype(jnp.int32) for turn in range(1, 1 << branch_level))
    home = ((held - WIDTH * part) << branch_level) + part
    order = jnp.where(lax.broadcasted_iota(jnp.int32, (channels, channels), 0) == home, 1.0, 0.0)
    return jnp.dot(
        order.astype(jnp.bfloat16),
        jnp.concatenate(parts, axis=0),
        preferred_element_type=jnp.float32,
    )


def turned(group, shift):
    shift = shift % LANES
    return pltpu.roll(group, shift, 1) if shift else group


def halo_kernel(
    container_ref, ext0, ext1, ext2, ext3, row_send, row_recv, col_send, col_recv, send_sem, recv_sem
):
    level = lax.axis_index("branch")
    place = lax.axis_index("row")
    col = lax.axis_index("col")
    row_count = lax.axis_size("row")
    col_count = lax.axis_size("col")
    up, down = place > 0, place < row_count - 1
    left, right = col > 0, col < col_count - 1
    above = (level, lax.rem(place + row_count - 1, row_count), col)
    below = (level, lax.rem(place + 1, row_count), col)
    west = (level, place, lax.rem(col + col_count - 1, col_count))
    east = (level, place, lax.rem(col + 1, col_count))
    neighbours = ((up, above), (down, below), (left, west), (right, east))

    barrier = pltpu.get_barrier_semaphore()
    for exists, device in neighbours:

        @pl.when(exists)
        def _():
            pl.semaphore_signal(barrier, inc=1, device_id=device, device_id_type=MESH)

    pl.semaphore_wait(barrier, sum(exists.astype(jnp.int32) for exists, _ in neighbours))

    def side_copy(rows, way):
        source, target = (row_send, row_recv) if way < 2 else (col_send, col_recv)
        return pltpu.make_async_remote_copy(
            src_ref=source.at[way % 2, 0:rows],
            dst_ref=target.at[1 - way % 2, 0:rows],
            send_sem=send_sem.at[way],
            recv_sem=recv_sem.at[way],
            device_id=neighbours[way][1],
            device_id_type=MESH,
        )

    lane = lax.broadcasted_iota(jnp.int32, (1, LANES), 1)

    def swap(rows, first_way):
        for way in (first_way, first_way + 1):

            @pl.when(neighbours[way][0])
            def _():
                side_copy(rows, way).start()

        received = row_recv if first_way == 0 else col_recv
        for way in (first_way, first_way + 1):
            exists = neighbours[first_way + 1 - way % 2][0]

            @pl.when(exists)
            def _():
                side_copy(rows, way).wait_recv()

            @pl.when(jnp.logical_not(exists))
            def _():
                received[1 - way % 2, 0:rows] = jnp.zeros((rows, LANES), jnp.bfloat16)

    def extend(branch_level, out_ref):
        channels, total = out_ref.shape
        rows, cols, pitch = TH >> branch_level, TW >> branch_level, row_pitch(branch_level)
        apart = cols * 2 >= LANES
        tile = natural_tile(branch_level, container_ref)

        def tile_row(y):
            at = y * cols
            low = at // LANES * LANES
            return tile[:, low : low + LANES], at - low

        for side, first in enumerate((0, rows - 2)):
            if apart:
                for turn in range(2):
                    group, at = tile_row(first + turn)
                    row_send[side, turn * channels : (turn + 1) * channels] = turned(
                        group, -at
                    ).astype(jnp.bfloat16)
            else:
                group, at = tile_row(first)
                row_send[side, 0:channels] = turned(group, -at).astype(jnp.bfloat16)
        swap(2 * channels if apart else channels, 0)

        def wide_row(r):
            if 2 <= r < rows + 2:
                return tile_row(r - 2)
            side, turn = (0, r) if r < 2 else (1, r - rows - 2)
            if apart:
                group = row_recv[side, turn * channels : (turn + 1) * channels]
                return group.astype(jnp.float32), 0
            return row_recv[side, 0:channels].astype(jnp.float32), turn * cols

        firsts = jnp.zeros((channels, LANES), jnp.float32)
        lasts = firsts
        for r in range(rows + 4):
            group, at = wide_row(r)
            here = lax.shift_right_logical(lane, 1) == r
            firsts = jnp.where(here, turned(group, 2 * r - at), firsts)
            lasts = jnp.where(here, turned(group, 2 * r - at - cols + 2), lasts)
        col_send[0, 0:channels] = firsts.astype(jnp.bfloat16)
        col_send[1, 0:channels] = lasts.astype(jnp.bfloat16)
        swap(channels, 2)
        from_west = col_recv[0, 0:channels].astype(jnp.float32)
        from_east = col_recv[1, 0:channels].astype(jnp.float32)

        groups = [None] * (total // LANES)

        def put(start, count, group, at):
            index, low = start // LANES, start % LANES
            group = turned(group, low - at)
            held = 0.0 if groups[index] is None else groups[index]
            groups[index] = (
                group
                if count == LANES
                else jnp.where((lane >= low) & (lane < low + count), group, held)
            )

        for r in range(rows + 4):
            put(r * pitch, cols, *wide_row(r))
            put(r * pitch + cols, 2, from_east, 2 * r)
            put((r - 1) % (rows + 4) * pitch + pitch - 2, 2, from_west, 2 * r)
        for index, group in enumerate(groups):
            out_ref[:, index * LANES : (index + 1) * LANES] = group.astype(jnp.bfloat16)

        for first_way, count in ((0, 2 * channels if apart else channels), (2, channels)):
            for way in (first_way, first_way + 1):

                @pl.when(neighbours[way][0])
                def _():
                    side_copy(count, way).wait_send()

    for branch_level, out_ref in enumerate((ext0, ext1, ext2, ext3)):
        pl.when(level == branch_level)(partial(extend, branch_level, out_ref))


def extended_tiles(container):
    vmem = pl.BlockSpec(memory_space=pltpu.VMEM)
    side = pltpu.VMEM((2, 8 * WIDTH, LANES), jnp.bfloat16)
    return pl.pallas_call(
        halo_kernel,
        out_shape=[
            jax.ShapeDtypeStruct((WIDTH << b, ((TH >> b) + 4) * row_pitch(b)), jnp.bfloat16)
            for b in range(4)
        ],
        in_specs=[vmem],
        out_specs=[vmem] * 4,
        scratch_shapes=[
            side,
            side,
            side,
            side,
            pltpu.SemaphoreType.DMA((4,)),
            pltpu.SemaphoreType.DMA((4,)),
        ],
        compiler_params=pltpu.CompilerParams(collective_id=1, has_side_effects=True),
        name="halo",
    )(container)


def tap_stack(field, pitch, rows_kept):
    total = field.shape[1]
    views = {}
    for dx in (-1, 0, 1):
        if pitch % LANES == 0:
            view = field if dx == 0 else pltpu.roll(field, -dx % total, 1)
            view = view.astype(jnp.bfloat16)
            if rows_kept:
                step = LANES
                view = jnp.concatenate(
                    [view[:, y * pitch : y * pitch + LANES] for y in range(1, rows_kept + 3)],
                    axis=1,
                )
                size = rows_kept * LANES
            else:
                step = pitch
                view = jnp.concatenate([view[:, total - pitch :], view, view[:, :pitch]], axis=1)
                size = total
            for dy in range(3):
                views[dy, dx] = view[:, dy * step : dy * step + size]
        else:
            for dy in range(3):
                shift = -(dx + (dy - 1) * pitch) % total
                view = field if shift == 0 else pltpu.roll(field, shift, 1)
                views[dy, dx] = view.astype(jnp.bfloat16)
    return jnp.concatenate([views[dy, dx] for dy in range(3) for dx in (-1, 0, 1)], axis=0)


def taps_of(weight_ref):
    if len(weight_ref.shape) == 2:
        return weight_ref[...]
    return jnp.concatenate([weight_ref[dy, dx] for dy in range(3) for dx in range(3)], axis=1)


def block_kernel(branch_level, ext_ref, first_ref, second_ref, bias_ref, strips_ref):
    pitch = row_pitch(branch_level)
    tile_rows, tile_cols = TH >> branch_level, TW >> branch_level
    channels, total = ext_ref.shape
    place, col = lax.axis_index("row"), lax.axis_index("col")
    field = ext_ref[...].astype(jnp.float32)
    first, second = taps_of(first_ref), taps_of(second_ref)
    hidden = jnp.dot(first, tap_stack(field, pitch, 0), preferred_element_type=jnp.float32)
    hidden = jnp.maximum(hidden + bias_ref[0], 0.0)
    pixel = lax.broadcasted_iota(jnp.int32, (1, total), 1) + 1
    y = lax.shift_right_logical(pixel, pitch.bit_length() - 1)
    x = pixel & (pitch - 1)
    top = jnp.where(place == 0, 1, -1)
    bottom = jnp.where(place == lax.axis_size("row") - 1, tile_rows + 2, -1)
    left = jnp.where(col == 0, 0, -1)
    right = jnp.where(col == lax.axis_size("col") - 1, tile_cols + 1, -1)
    inside = (y != top) & (y != bottom) & (x != left) & (x != right)
    hidden = jnp.where(inside, hidden, 0.0).astype(jnp.bfloat16).astype(jnp.float32)
    narrow = tile_cols == LANES
    rows_kept = tile_rows if narrow else 0
    after = jnp.dot(
        second, tap_stack(hidden, pitch, rows_kept), preferred_element_type=jnp.float32
    )
    if narrow:
        field = jnp.concatenate(
            [field[:, y * pitch : y * pitch + LANES] for y in range(2, tile_rows + 2)], axis=1
        )
    settled = jnp.maximum(after + bias_ref[1] + field, 0.0)
    strip_rows = tile_rows // STRIPS
    lane = lax.broadcasted_iota(jnp.int32, (1, LANES), 1)
    for strip in range(STRIPS):
        groups = []
        if narrow:
            groups = [
                settled[:, y * LANES : (y + 1) * LANES]
                for y in range(strip * strip_rows, (strip + 1) * strip_rows)
            ]
        else:
            per_group = min(LANES // tile_cols, strip_rows)
            for start in range(0, strip_rows, per_group):
                merged = None
                for turn in range(per_group):
                    at = (strip * strip_rows + start + turn + 2) * pitch
                    part = settled[:, at // LANES * LANES : at // LANES * LANES + LANES]
                    shift = (turn * tile_cols - at) % LANES
                    part = pltpu.roll(part, shift, 1) if shift else part
                    merged = part if turn == 0 else jnp.where(lane < turn * tile_cols, merged, part)
                groups.append(merged)
        for at, group in enumerate(groups):
            strips_ref[strip, at * channels : (at + 1) * channels] = group.astype(jnp.bfloat16)


def deep_block(branch_level, tiles, kernels, biases):
    channels = WIDTH << branch_level
    extended = tiles[branch_level]
    if channels == kernels.shape[-1] and channels % LANES == 0:
        first, second = kernels[0], kernels[1]
    else:
        first, second = (
            jnp.concatenate(
                [
                    kernels[layer, dy, dx, :channels, :channels]
                    for dy in range(3)
                    for dx in range(3)
                ],
                axis=1,
            )
            for layer in range(2)
        )
    vmem = pl.BlockSpec(memory_space=pltpu.VMEM)
    return pl.pallas_call(
        partial(block_kernel, branch_level),
        out_shape=jax.ShapeDtypeStruct((STRIPS, PIECE_ROWS, LANES), jnp.bfloat16),
        in_specs=[vmem] * 4,
        out_specs=vmem,
        compiler_params=pltpu.CompilerParams(vmem_limit_bytes=60 << 20),
        name=f"block_{branch_level}",
    )(extended, first, second, biases[:, :channels, None])


LANES = 128
STRIPS = 4
PIECE_ROWS = WIDTH * TH * TW // (STRIPS * LANES)
MESH = pl.DeviceIdType.MESH


def piece_rows(branch_level):
    pixels = TH * TW // STRIPS >> 2 * branch_level
    return (WIDTH << branch_level) * max(1, pixels // LANES)


def block_mask(fine_level, coarse_level):
    fine_cols = TW >> fine_level
    coarse_cols = TW >> coarse_level
    fine = TH * TW // STRIPS >> 2 * fine_level
    coarse = TH * TW // STRIPS >> 2 * coarse_level
    shift = coarse_level - fine_level
    pixel = lax.broadcasted_iota(jnp.int32, (fine, 1), 0)
    row = lax.shift_right_logical(pixel, fine_cols.bit_length() - 1 + shift)
    col = lax.shift_right_logical(pixel & (fine_cols - 1), shift)
    home = row * coarse_cols + col
    target = lax.broadcasted_iota(jnp.int32, (fine, coarse), 1)
    return jnp.where(home == target, 1.0, 0.0).astype(jnp.bfloat16)


def mixed(weight_ref, target, source, tile_data):
    start = ((1 << source) - 1) * WIDTH
    low = start // LANES * LANES
    high = min(-(-(start + tile_data.shape[0]) // LANES) * LANES, weight_ref.shape[1])
    pieces = []
    if start > low:
        pieces.append(jnp.zeros((start - low, tile_data.shape[1]), tile_data.dtype))
    pieces.append(tile_data)
    if high > start + tile_data.shape[0]:
        pieces.append(
            jnp.zeros((high - start - tile_data.shape[0], tile_data.shape[1]), tile_data.dtype)
        )
    rows = ((1 << target) - 1) * WIDTH
    return jnp.dot(
        weight_ref[rows : rows + (WIDTH << target), low:high],
        jnp.concatenate(pieces, axis=0),
        preferred_element_type=jnp.float32,
    ).astype(jnp.bfloat16)


def join_strip(maps, masks, weight_ref, bias_ref, out_refs):
    for target in range(4):
        start = ((1 << target) - 1) * WIDTH
        total = maps[target].astype(jnp.float32) + bias_ref[start : start + (WIDTH << target), :]
        for source in range(4):
            if source < target:
                share = 0.25 ** (target - source)
                shrunk = jnp.dot(
                    maps[source], masks[source, target], preferred_element_type=jnp.float32
                )
                term = mixed(weight_ref, target, source, (shrunk * share).astype(jnp.bfloat16))
                total = total + term.astype(jnp.float32)
            elif source > target:
                term = mixed(weight_ref, target, source, maps[source])
                total = total + lax.dot_general(
                    term,
                    masks[target, source],
                    (((1,), (1,)), ((), ())),
                    preferred_element_type=jnp.float32,
                )
        out_refs[target][...] = jnp.maximum(total, 0.0).astype(jnp.bfloat16)


def exchange_join(
    strips_ref, weight_ref, bias_ref, out0, out1, out2, out3, held, send_sem, recv_sem, own_sem
):
    level = lax.axis_index("branch")
    place = lax.axis_index("row")
    col = lax.axis_index("col")
    home = level == place

    barrier = pltpu.get_barrier_semaphore()
    for other in range(4):

        @pl.when(jnp.logical_not(home & (level == other)))
        def _():
            pl.semaphore_signal(
                barrier, inc=1, device_id=(other, level, col), device_id_type=MESH
            )

    pl.semaphore_wait(barrier, jnp.where(home, 3, 4))

    def remote(source, strip):
        rows = piece_rows(source)
        return pltpu.make_async_remote_copy(
            src_ref=strips_ref.at[strip, 0:rows],
            dst_ref=held.at[source, 0:rows],
            send_sem=send_sem.at[strip],
            recv_sem=recv_sem.at[source],
            device_id=(place, strip, col),
            device_id_type=MESH,
        )

    def own(source):
        rows = piece_rows(source)
        return pltpu.make_async_copy(
            strips_ref.at[source, 0:rows], held.at[source, 0:rows], own_sem
        )

    for source in range(4):
        for step in range(4):
            strip = (source + 1 + step) % 4

            @pl.when((level == source) & jnp.logical_not(home & (level == strip)))
            def _():
                remote(source, strip).start()

        @pl.when((level == source) & home)
        def _():
            own(source).start()

    masks = {
        (fine, coarse): block_mask(fine, coarse)
        for fine in range(3)
        for coarse in range(fine + 1, 4)
    }

    for source in range(4):

        @pl.when(jnp.logical_not(home & (level == source)))
        def _():
            remote(source, 0).wait_recv()

        @pl.when((level == source) & home)
        def _():
            own(source).wait()

    maps = []
    for source in range(4):
        channels = WIDTH << source
        pixels = TH * TW // STRIPS >> 2 * source
        if pixels >= LANES:
            maps.append(
                jnp.concatenate(
                    [
                        held[source, at * channels : (at + 1) * channels]
                        for at in range(pixels // LANES)
                    ],
                    axis=1,
                )
            )
        else:
            maps.append(held[source, 0:channels][:, :pixels])
    join_strip(maps, masks, weight_ref, bias_ref, (out0, out1, out2, out3))

    for source in range(4):
        for strip in range(4):

            @pl.when((level == source) & jnp.logical_not(home & (level == strip)))
            def _():
                remote(source, strip).wait_send()


def joined(strips, join_weight, join_bias):
    vmem = pl.BlockSpec(memory_space=pltpu.VMEM)
    return pl.pallas_call(
        exchange_join,
        out_shape=[
            jax.ShapeDtypeStruct(
                (WIDTH << b, TH * TW // STRIPS >> 2 * b), jnp.bfloat16
            )
            for b in range(4)
        ],
        in_specs=[vmem] * 3,
        out_specs=[vmem] * 4,
        scratch_shapes=[
            pltpu.VMEM((4, PIECE_ROWS, LANES), jnp.bfloat16),
            pltpu.SemaphoreType.DMA((4,)),
            pltpu.SemaphoreType.DMA((4,)),
            pltpu.SemaphoreType.DMA,
        ],
        compiler_params=pltpu.CompilerParams(collective_id=0, has_side_effects=True),
        name="exchange_join",
    )(strips, join_weight, join_bias[:, None])


def local(section_in, conv_weight, conv_bias, join_weight, join_bias):
    level_index = lax.axis_index("branch")
    container = section_in[0, 0, 0]
    kernels = conv_weight[0]
    biases = conv_bias[0]
    tiles = extended_tiles(container)
    strips = lax.switch(
        level_index,
        [partial(deep_block, branch_level) for branch_level in range(4)],
        tiles,
        kernels,
        biases,
    )
    outs = joined(strips, join_weight, join_bias)
    return tuple(
        out.reshape(WIDTH << b, (TH >> b) // STRIPS, TW >> b) for b, out in enumerate(outs)
    )


def solution(mesh):
    in_specs = (
        P("branch", "row", "col", None, None),
        P("branch", None, None, None, None, None),
        P("branch", None, None),
        P(),
        P(),
    )
    out_specs = (
        P(None, ("branch", "row"), "col"),
        P(None, ("branch", "row"), "col"),
        P(None, ("branch", "row"), "col"),
        P(None, ("branch", "row"), "col"),
    )
    return jax.shard_map(local, mesh=mesh, in_specs=in_specs, out_specs=out_specs, check_vma=False)
```

profile of v0, /device:TPU:29, one launch (start us, length us, event | category | flops | bytes accessed | tf_op | source)
XLA Modules:
  0.0 56.7 jit_solution(5201975177441725303)
XLA Ops:
  0.6 11.4 %halo.1 = (bf16[48,9216]{1,0:T(8,128)(2,1)S(1)}, bf16[96,2560]{1,0:T(8,128)(2,1)S(1)}, bf16[192,768]{1,0:T(8,128)(2,1)S(1)}, bf16[384,256]{1,0:T(8,128)(2,1)S(1)}) custom-call(bf16[48,4096]{1,0:T(8,128)(2,1)} %bitcast.131), custom_call_target="tpu_custom_call" | custom-call | tf_op jit(solution)/shard_map/halo/pallas_call | solution.py:183
  12.1 0.0 copy-start.2
  12.1 12.9 %conditional.1 = (bf16[4,384,128]{2,1,0:T(8,128)(2,1)S(1)}) conditional(s32[]{:T(128)} %clamp.3, (bf16[2,3,3,384,384]{4,3,2,1,0:T(8,128)(2,1)}, f32[2,384]{1,0:T(2,128)}, bf16[48,9216]{1,0:T(8,128)(2,1)S(1)}) %tuple.87, (bf16[2,3,3,384,384]{4,3,2,1,0:T(8,128)(2,1)}, f32[2,384]{1,0:T(2,128)}, ...), branch_computations={%region_0.0_spmd, %region_1.0_spmd, %region_2.0_spmd, %region_3.0_... | conditional | bytes 10635300 | solution.py:505
  12.3 0.0 copy-start.1
  12.3 5.6 %slice_bitcast_fusion.57 = (bf16[3,3,384,384]{3,2,1,0:T(8,128)(2,1)}, bf16[3,3,384,384]{3,2,1,0:T(8,128)(2,1)}) fusion(bf16[2,3,3,384,384]{4,3,2,1,0:T(8,128)(2,1)} %get-tuple-element.39), kind=kLoop, calls=%fused_computation.57 | loop fusion | bytes 10616832 | tf_op jit(solution)/shard_map/cond/branch_3_fun/squeeze | solution.py:294
  17.9 0.0 copy-done.1
  17.9 1.0 %copy.16.bias_ref = f32[2,384,1]{2,1,0:T(8,128)} copy(f32[2,384,1]{1,0,2:T(2,128)S(1)} %bitcast.140) | data formatting | bytes 6144 | tf_op jit(solution)/shard_map/cond/branch_3_fun/broadcast_in_dim;squeeze | solution.py:315
  18.9 5.9 %block_3.1 = bf16[4,384,128]{2,1,0:T(8,128)(2,1)S(1)} custom-call(bf16[384,256]{1,0:T(8,128)(2,1)S(1)} %get-tuple-element.38.ext_ref, bf16[3,3,384,384]{3,2,1,0:T(8,128)(2,1)} %get-tuple-element.124.first_ref, bf16[3,3,384,384]{3,2,1,0:T(8,128)(2,1)} %get-tuple-element.123.second_ref, f32[2,384,1]{2,1,0:T(8,128)} %copy.16.bias_ref), custom_call_target="tpu_custom_call" | custom-call | tf_op jit(solution)/shard_map/cond/branch_3_fun/block_3/pallas_call | solution.py:308
  25.0 0.0 copy-done.2
  25.0 0.9 %broadcast_in_dim.13.bias_ref = f32[720,1]{1,0:T(8,128)} reshape(f32[720]{0:T(1024)S(1)} %copy-done.2) | data formatting | bytes 5760 | tf_op jit(solution)/shard_map/broadcast_in_dim | solution.py:496
  25.9 24.7 %exchange_join.1 = (bf16[48,1024]{1,0:T(8,128)(2,1)}, bf16[96,256]{1,0:T(8,128)(2,1)}, bf16[192,64]{1,0:T(8,128)(2,1)}, bf16[384,16]{1,0:T(8,128)(2,1)}) custom-call(bf16[4,384,128]{2,1,0:T(8,128)(2,1)S(1)} %get-tuple-element.125.strips_ref, bf16[720,720]{1,0:T(8,128)(2,1)} %weight_ref.1, f32[720,1]{1,0:T(8,128)} %broadcast_in_dim.13.bias_ref), custom_call_target="tpu_custom_call" | custom-call | tf_op jit(solution)/shard_map/exchange_join/pallas_call | solution.py:478
  50.5 1.5 %copy.21 = bf16[6,8,8,128]{3,2,1,0:T(8,128)(2,1)} copy(bf16[6,8,8,128]{3,1,2,0:T(8,128)(2,1)} %bitcast.134) | data formatting | bytes 196608
  52.1 1.5 %copy.18 = bf16[96,256]{0,1:T(8,128)(2,1)} copy(bf16[96,256]{1,0:T(8,128)(2,1)} %get-tuple-element.58) | data formatting | bytes 98304 | tf_op jit(solution)/shard_map/exchange_join/pallas_call | solution.py:478
  53.6 1.5 %copy.19 = bf16[192,64]{0,1:T(8,128)(2,1)} copy(bf16[192,64]{1,0:T(8,128)(2,1)} %get-tuple-element.59) | data formatting | bytes 49152 | tf_op jit(solution)/shard_map/exchange_join/pallas_call | solution.py:478
  55.1 1.6 %copy.20 = bf16[384,1,16]{0,2,1:T(8,128)(2,1)} copy(bf16[384,1,16]{2,0,1:T(8,128)(2,1)} %bitcast.133) | data formatting | bytes 24576
Async XLA Ops:
  12.1 12.9 %copy-start.2 = (f32[720]{0:T(1024)S(1)}, f32[720]{0:T(1024)}, u32[]{:S(2)}) copy-start(f32[720]{0:T(1024)} %param.13) | copy-start | bytes 8644
  12.3 5.6 %copy-start.1 = (f32[1,2,384]{2,1,0:T(2,128)S(1)}, f32[1,2,384]{2,1,0:T(2,128)}, u32[]{:S(2)}) copy-start(f32[1,2,384]{2,1,0:T(2,128)} %get-tuple-element.40) | copy-start | bytes 9220 | tf_op jit(solution)/shard_map/cond
where the time goes:
time: 57.2 us; the launch traced here: 56.7 us
  Pallas kernels  42 us (73%)
  local copies, waits for them, and re-layouts  13.6 us (24%)
  between operations  0.68 us (1%)
    pallas_call x1, Pallas kernels, joined(): pl.pallas_call(exchange_join, out_shape=[jax.ShapeDtypeStruct((WIDTH << b...  24.7 us
    pallas_call x1, Pallas kernels, extended_tiles(): pl.pallas_call(halo_kernel, out_shape=[jax.ShapeDtypeStruct((WIDTH << b,...  11.4 us
    pallas_call x1, Pallas kernels, deep_block(): pl.pallas_call(partial(block_kernel, branch_level), out_shape=jax.ShapeDt...  5.87 us
    squeeze x1, local copies, waits for them, and re-layouts, deep_block(): first, second = (kernels[0], kernels[1])  5.57 us
    unnamed x4, local copies, waits for them, and re-layouts  3.12 us
    pallas_call x2, local copies, waits for them, and re-layouts, joined(): pl.pallas_call(exchange_join, out_shape=[jax.ShapeDtypeStruct((WIDTH << b...  3.03 us

commit v1 on v0

--- a/solution.py
+++ b/solution.py
@@ -229,19 +229,34 @@
     return jnp.concatenate([views[dy, dx] for dy in range(3) for dx in (-1, 0, 1)], axis=0)
 
 
-def taps_of(weight_ref):
-    if len(weight_ref.shape) == 2:
-        return weight_ref[...]
-    return jnp.concatenate([weight_ref[dy, dx] for dy in range(3) for dx in range(3)], axis=1)
-
-
-def block_kernel(branch_level, ext_ref, first_ref, second_ref, bias_ref, strips_ref):
+def taps_of(weight_refs, layer):
+    if len(weight_refs) == 2:
+        return weight_refs[layer][...]
+    (weight_ref,) = weight_refs
+    return jnp.concatenate(
+        [weight_ref[layer, dy, dx] for dy in range(3) for dx in range(3)], axis=1
+    )
+
+
+def folded(group, pixels):
+    folds = LANES // pixels
+    size = group.shape[0] // folds
+    lane = lax.broadcasted_iota(jnp.int32, (1, LANES), 1)
+    merged = group[:size]
+    for turn in range(1, folds):
+        part = turned(group[turn * size : (turn + 1) * size], turn * pixels)
+        merged = jnp.where(lane < turn * pixels, merged, part)
+    return [merged]
+
+
+def block_kernel(branch_level, ext_ref, bias_ref, *refs):
+    weight_refs, strips_ref = refs[:-1], refs[-1]
     pitch = row_pitch(branch_level)
     tile_rows, tile_cols = TH >> branch_level, TW >> branch_level
     channels, total = ext_ref.shape
     place, col = lax.axis_index("row"), lax.axis_index("col")
     field = ext_ref[...].astype(jnp.float32)
-    first, second = taps_of(first_ref), taps_of(second_ref)
+    first, second = taps_of(weight_refs, 0), taps_of(weight_refs, 1)
     hidden = jnp.dot(first, tap_stack(field, pitch, 0), preferred_element_type=jnp.float32)
     hidden = jnp.maximum(hidden + bias_ref[0], 0.0)
     pixel = lax.broadcasted_iota(jnp.int32, (1, total), 1) + 1
@@ -283,17 +298,20 @@
                     part = pltpu.roll(part, shift, 1) if shift else part
                     merged = part if turn == 0 else jnp.where(lane < turn * tile_cols, merged, part)
                 groups.append(merged)
+        if len(groups) == 1:
+            groups = folded(groups[0], strip_rows * tile_cols)
+        size = groups[0].shape[0]
         for at, group in enumerate(groups):
-            strips_ref[strip, at * channels : (at + 1) * channels] = group.astype(jnp.bfloat16)
+            strips_ref[strip, at * size : (at + 1) * size] = group.astype(jnp.bfloat16)
 
 
 def deep_block(branch_level, tiles, kernels, biases):
     channels = WIDTH << branch_level
     extended = tiles[branch_level]
     if channels == kernels.shape[-1] and channels % LANES == 0:
-        first, second = kernels[0], kernels[1]
+        weights = [kernels]
     else:
-        first, second = (
+        weights = [
             jnp.concatenate(
                 [
                     kernels[layer, dy, dx, :channels, :channels]
@@ -303,16 +321,16 @@
                 axis=1,
             )
             for layer in range(2)
-        )
+        ]
     vmem = pl.BlockSpec(memory_space=pltpu.VMEM)
     return pl.pallas_call(
         partial(block_kernel, branch_level),
         out_shape=jax.ShapeDtypeStruct((STRIPS, PIECE_ROWS, LANES), jnp.bfloat16),
-        in_specs=[vmem] * 4,
+        in_specs=[vmem] * (2 + len(weights)),
         out_specs=vmem,
         compiler_params=pltpu.CompilerParams(vmem_limit_bytes=60 << 20),
         name=f"block_{branch_level}",
-    )(extended, first, second, biases[:, :channels, None])
+    )(extended, biases[:, :channels, None], *weights)
 
 
 LANES = 128
@@ -322,8 +340,7 @@
 
 
 def piece_rows(branch_level):
-    pixels = TH * TW // STRIPS >> 2 * branch_level
-    return (WIDTH << branch_level) * max(1, pixels // LANES)
+    return PIECE_ROWS >> branch_level
 
 
 def block_mask(fine_level, coarse_level):
@@ -380,73 +397,97 @@
                     (((1,), (1,)), ((), ())),
                     preferred_element_type=jnp.float32,
                 )
-        out_refs[target][...] = jnp.maximum(total, 0.0).astype(jnp.bfloat16)
-
-
-def exchange_join(
-    strips_ref, weight_ref, bias_ref, out0, out1, out2, out3, held, send_sem, recv_sem, own_sem
+        total = jnp.maximum(total, 0.0)
+        out_ref = out_refs[target]
+        if len(out_ref.shape) == 2:
+            out_ref[...] = total.T.astype(jnp.bfloat16)
+        else:
+            lines = [total[:, at : at + LANES] for at in range(0, total.shape[1], LANES)]
+            out_ref[...] = jnp.stack(lines, axis=1).astype(jnp.bfloat16)
+
+
+def exchange_kernel(
+    strips_ref, held, relay, near_send, near_recv, far_send, far_recv, own_sem
 ):
     level = lax.axis_index("branch")
     place = lax.axis_index("row")
     col = lax.axis_index("col")
+    size = STRIPS
     home = level == place
 
     barrier = pltpu.get_barrier_semaphore()
-    for other in range(4):
-
-        @pl.when(jnp.logical_not(home & (level == other)))
-        def _():
-            pl.semaphore_signal(
-                barrier, inc=1, device_id=(other, level, col), device_id_type=MESH
-            )
-
-    pl.semaphore_wait(barrier, jnp.where(home, 3, 4))
-
-    def remote(source, strip):
-        rows = piece_rows(source)
+    for step in range(1, size):
+        for device in (
+            (level, lax.rem(place + step, size), col),
+            (lax.rem(level + step, size), place, col),
+        ):
+            pl.semaphore_signal(barrier, inc=1, device_id=device, device_id_type=MESH)
+    pl.semaphore_wait(barrier, 2 * (size - 1))
+
+    def near(rows, step):
+        strip = lax.rem(place + step, size)
         return pltpu.make_async_remote_copy(
             src_ref=strips_ref.at[strip, 0:rows],
-            dst_ref=held.at[source, 0:rows],
-            send_sem=send_sem.at[strip],
-            recv_sem=recv_sem.at[source],
-            device_id=(place, strip, col),
+            dst_ref=relay.at[step - 1, 0:rows],
+            send_sem=near_send.at[step - 1],
+            recv_sem=near_recv.at[step - 1],
+            device_id=(level, strip, col),
             device_id_type=MESH,
         )
 
-    def own(source):
+    def far(source, step):
         rows = piece_rows(source)
-        return pltpu.make_async_copy(
-            strips_ref.at[source, 0:rows], held.at[source, 0:rows], own_sem
+        tile = lax.rem(place + size - step, size)
+        piece = strips_ref.at[place, 0:rows] if step == 0 else relay.at[step - 1, 0:rows]
+        return (
+            tile,
+            pltpu.make_async_remote_copy(
+                src_ref=piece,
+                dst_ref=held.at[source, 0:rows],
+                send_sem=far_send.at[step],
+                recv_sem=far_recv.at[source],
+                device_id=(tile, place, col),
+                device_id_type=MESH,
+            ),
+            pltpu.make_async_copy(piece, held.at[source, 0:rows], own_sem),
         )
 
-    for source in range(4):
-        for step in range(4):
-            strip = (source + 1 + step) % 4
-
-            @pl.when((level == source) & jnp.logical_not(home & (level == strip)))
-            def _():
-                remote(source, strip).start()
-
-        @pl.when((level == source) & home)
-        def _():
-            own(source).start()
-
+    def onward(source):
+        rows = piece_rows(source)
+        for step in (2, 1, 3):
+            near(rows, step).start()
+        for step in (0, 1, 3, 2):
+            if step:
+                near(rows, step).wait_recv()
+            tile, remote, own = far(source, step)
+            pl.when(tile != level)(remote.start)
+            pl.when(tile == level)(own.start)
+
+    for source in range(size):
+        pl.when(level == source)(partial(onward, source))
+
+    for source in range(size):
+        _, remote, own = far(source, 0)
+        pl.when(level != source)(remote.wait_recv)
+        pl.when(level == source)(own.wait)
+
+    def sent(source):
+        for step in range(1, size):
+            near(piece_rows(source), step).wait_send()
+        for step in range(size):
+            tile, remote, _ = far(source, step)
+            pl.when(tile != level)(remote.wait_send)
+
+    for source in range(size):
+        pl.when(level == source)(partial(sent, source))
+
+
+def join_kernel(held, weight_ref, bias_ref, *out_refs):
     masks = {
         (fine, coarse): block_mask(fine, coarse)
         for fine in range(3)
         for coarse in range(fine + 1, 4)
     }
-
-    for source in range(4):
-
-        @pl.when(jnp.logical_not(home & (level == source)))
-        def _():
-            remote(source, 0).wait_recv()
-
-        @pl.when((level == source) & home)
-        def _():
-            own(source).wait()
-
     maps = []
     for source in range(4):
         channels = WIDTH << source
@@ -462,38 +503,49 @@
                 )
             )
         else:
-            maps.append(held[source, 0:channels][:, :pixels])
-    join_strip(maps, masks, weight_ref, bias_ref, (out0, out1, out2, out3))
-
-    for source in range(4):
-        for strip in range(4):
-
-            @pl.when((level == source) & jnp.logical_not(home & (level == strip)))
-            def _():
-                remote(source, strip).wait_send()
+            piece = held[source, 0 : piece_rows(source)].astype(jnp.float32)
+            unfolded = jnp.concatenate(
+                [turned(piece, -turn * pixels) for turn in range(LANES // pixels)], axis=0
+            )
+            maps.append(unfolded.astype(jnp.bfloat16)[:, :pixels])
+    join_strip(maps, masks, weight_ref, bias_ref, out_refs)
 
 
 def joined(strips, join_weight, join_bias):
     vmem = pl.BlockSpec(memory_space=pltpu.VMEM)
-    return pl.pallas_call(
-        exchange_join,
+    held = pl.pallas_call(
+        exchange_kernel,
+        out_shape=jax.ShapeDtypeStruct((STRIPS, PIECE_ROWS, LANES), jnp.bfloat16),
+        in_specs=[vmem],
+        out_specs=vmem,
+        scratch_shapes=[
+            pltpu.VMEM((STRIPS - 1, PIECE_ROWS, LANES), jnp.bfloat16),
+            pltpu.SemaphoreType.DMA((STRIPS - 1,)),
+            pltpu.SemaphoreType.DMA((STRIPS - 1,)),
+            pltpu.SemaphoreType.DMA((STRIPS,)),
+            pltpu.SemaphoreType.DMA((STRIPS,)),
+            pltpu.SemaphoreType.DMA,
+        ],
+        compiler_params=pltpu.CompilerParams(collective_id=0, has_side_effects=True),
+        name="exchange",
+    )(strips)
+    shapes = [(WIDTH << b, (TH >> b) // STRIPS, TW >> b) for b in range(4)]
+    outs = pl.pallas_call(
+        join_kernel,
         out_shape=[
             jax.ShapeDtypeStruct(
-                (WIDTH << b, TH * TW // STRIPS >> 2 * b), jnp.bfloat16
+                shape if shape[2] == LANES else (shape[1] * shape[2], shape[0]), jnp.bfloat16
             )
-            for b in range(4)
+            for shape in shapes
         ],
         in_specs=[vmem] * 3,
         out_specs=[vmem] * 4,
-        scratch_shapes=[
-            pltpu.VMEM((4, PIECE_ROWS, LANES), jnp.bfloat16),
-            pltpu.SemaphoreType.DMA((4,)),
-            pltpu.SemaphoreType.DMA((4,)),
-            pltpu.SemaphoreType.DMA,
-        ],
-        compiler_params=pltpu.CompilerParams(collective_id=0, has_side_effects=True),
-        name="exchange_join",
-    )(strips, join_weight, join_bias[:, None])
+        name="join",
+    )(held, join_weight, join_bias[:, None])
+    return tuple(
+        out if out.ndim == 3 else out.reshape(*shape[1:], shape[0]).transpose(2, 0, 1)
+        for out, shape in zip(outs, shapes)
+    )
 
 
 def local(section_in, conv_weight, conv_bias, join_weight, join_bias):
@@ -509,10 +561,7 @@
         kernels,
         biases,
     )
-    outs = joined(strips, join_weight, join_bias)
-    return tuple(
-        out.reshape(WIDTH << b, (TH >> b) // STRIPS, TW >> b) for b, out in enumerate(outs)
-    )
+    return tuple(joined(strips, join_weight, join_bias))
 
 
 def solution(mesh):

time: 57.2 us -> 42.2 us (0.74)
  the two profiles are of different devices: /device:TPU:29 before, /device:TPU:0 now
where the time goes in v1:
time: 42.2 us; the launch traced here: 41.9 us
  Pallas kernels  36.5 us (86%)
  local copies, waits for them, and re-layouts  4.69 us (11%)
  between operations  0.68 us (2%)
    pallas_call x1, Pallas kernels, joined(): pl.pallas_call(exchange_kernel, out_shape=jax.ShapeDtypeStruct((STRIPS, P...  20.7 us
    pallas_call x1, Pallas kernels, extended_tiles(): pl.pallas_call(halo_kernel, out_shape=[jax.ShapeDtypeStruct((WIDTH << b,...  8.51 us
    pallas_call x1, Pallas kernels, joined(): pl.pallas_call(join_kernel, out_shape=[jax.ShapeDtypeStruct(shape if shap...  4.27 us
    pallas_call x1, Pallas kernels, deep_block(): pl.pallas_call(partial(block_kernel, branch_level), out_shape=jax.ShapeDt...  3 us
    concatenate x2, local copies, waits for them, and re-layouts, deep_block(): jnp.concatenate([kernels[layer, dy, dx, :channels, :channels] for dy in r...  1.47 us
    broadcast_in_dim x2, local copies, waits for them, and re-layouts, deep_block(): biases[:, :channels, None]  1.4 us
    squeeze x1, local copies, waits for them, and re-layouts, deep_block(): kernels[layer, dy, dx, :channels, :channels]  0.91 us
    broadcast_in_dim x1, local copies, waits for them, and re-layouts, joined(): join_bias[:, None]  0.89 us

profile of v1, /device:TPU:0, one launch (start us, length us, event | category | flops | bytes accessed | tf_op | source)
XLA Modules:
  0.0 41.9 jit_solution(17484092342283918625)
XLA Ops:
  0.6 8.5 %halo.1 = (bf16[48,9216]{1,0:T(8,128)(2,1)S(1)}, bf16[96,2560]{1,0:T(8,128)(2,1)S(1)}, bf16[192,768]{1,0:T(8,128)(2,1)S(1)}, bf16[384,256]{1,0:T(8,128)(2,1)S(1)}) custom-call(bf16[48,4096]{1,0:T(8,128)(2,1)} %bitcast.131), custom_call_target="tpu_custom_call" | custom-call | tf_op jit(solution)/shard_map/halo/pallas_call | solution.py:183
  9.1 0.0 copy-start.1
  9.2 6.8 %conditional.1 = (bf16[4,384,128]{2,1,0:T(8,128)(2,1)S(1)}) conditional(s32[]{:T(128)} %clamp.3, (f32[2,384]{1,0:T(2,128)}, bf16[2,3,3,384,384]{4,3,2,1,0:T(8,128)(2,1)}, bf16[48,9216]{1,0:T(8,128)(2,1)S(1)}) %tuple.84, (f32[2,384]{1,0:T(2,128)}, bf16[2,3,3,384,384]{4,3,2,1,0:T(8,128)(2,1)}, ...), branch_computations={%region_0.0_spmd, %region_1.0_spmd, %region_2.0_spmd, %region_3.0_... | conditional | bytes 5326884 | solution.py:557
  9.2 0.9 %slice_bitcast_fusion = (bf16[48,48]{1,0:T(8,128)(2,1)S(1)}, bf16[48,48]{1,0:T(8,128)(2,1)S(1)}, bf16[48,48]{1,0:T(8,128)(2,1)S(1)}, bf16[48,48]{1,0:T(8,128)(2,...) fusion(bf16[2,3,3,384,384]{4,3,2,1,0:T(8,128)(2,1)} %get-tuple-, ...), kind=kLoop, calls=%fused_computation | loop fusion | bytes 165888 | tf_op jit(solution)/shard_map/cond/branch_0_fun/squeeze | solution.py:317
  10.1 0.7 %concatenate.13.refs_1_ = bf16[48,432]{1,0:T(8,128)(2,1)} concatenate(bf16[48,48]{1,0:T(8,128)(2,1)S(1)} %get-tuple-element.69, bf16[48,48]{1,0:T(8,128)(2,1)S(1)} %get-tuple-element.68, bf16[48,48]{1,0:T(8,128)(2,1)S(1)} %get-tuple-element.67, bf16[48,48]{1,0:T(8,128)(2,1)S(1)} %get-tuple-element.66, bf16[48,48]{1,0:T(8,128)(2,1)S(1)} %get-tuple-element.65, ...), dimensions={1} | concatenate | bytes 82944 | tf_op jit(solution)/shard_map/cond/branch_0_fun/concatenate | solution.py:315
  10.8 0.7 %concatenate.12.refs_0_ = bf16[48,432]{1,0:T(8,128)(2,1)} concatenate(bf16[48,48]{1,0:T(8,128)(2,1)S(1)} %get-tuple-element.78, bf16[48,48]{1,0:T(8,128)(2,1)S(1)} %get-tuple-element.77, bf16[48,48]{1,0:T(8,128)(2,1)S(1)} %get-tuple-element.76, bf16[48,48]{1,0:T(8,128)(2,1)S(1)} %get-tuple-element.75, bf16[48,48]{1,0:T(8,128)(2,1)S(1)} %get-tuple-element.74, ...), dimensions={1} | concatenate | bytes 82944 | tf_op jit(solution)/shard_map/cond/branch_0_fun/concatenate | solution.py:315
  11.6 0.7 %slice_bitcast_fusion.18 = f32[2,48,1]{1,0,2:T(2,128)S(1)} fusion(f32[2,384]{1,0:T(2,128)} %get-tuple-element.26), kind=kLoop, calls=%fused_computation.18 | loop fusion | bytes 768 | tf_op jit(solution)/shard_map/cond/branch_0_fun/broadcast_in_dim | solution.py:333
  12.2 0.7 %copy.10.bias_ref = f32[2,48,1]{2,1,0:T(8,128)} copy(f32[2,48,1]{1,0,2:T(2,128)S(1)} %slice_bitcast_fusion.18) | data formatting | bytes 768 | tf_op jit(solution)/shard_map/cond/branch_0_fun/broadcast_in_dim | solution.py:333
  13.0 3.0 %block_0.1 = bf16[4,384,128]{2,1,0:T(8,128)(2,1)S(1)} custom-call(bf16[48,9216]{1,0:T(8,128)(2,1)S(1)} %get-tuple-element.25.ext_ref, f32[2,48,1]{2,1,0:T(8,128)} %copy.10.bias_ref, bf16[48,432]{1,0:T(8,128)(2,1)} %concatenate.12.refs_0_, bf16[48,432]{1,0:T(8,128)(2,1)} %concatenate.13.refs_1_), custom_call_target="tpu_custom_call" | custom-call | tf_op jit(solution)/shard_map/cond/branch_0_fun/block_0/pallas_call | solution.py:326
  16.0 20.7 %exchange.1.held = bf16[4,384,128]{2,1,0:T(8,128)(2,1)} custom-call(bf16[4,384,128]{2,1,0:T(8,128)(2,1)S(1)} %get-tuple-element.115.strips_ref), custom_call_target="tpu_custom_call" | custom-call | tf_op jit(solution)/shard_map/exchange/pallas_call | solution.py:516
  36.7 0.0 copy-done.1
  36.7 0.9 %broadcast_in_dim.13.bias_ref = f32[720,1]{1,0:T(8,128)} reshape(f32[720]{0:T(1024)S(1)} %copy-done.1) | data formatting | bytes 5760 | tf_op jit(solution)/shard_map/broadcast_in_dim | solution.py:544
  37.6 4.3 %join.1 = (bf16[48,8,128]{2,1,0:T(8,128)(2,1)}, bf16[256,96]{1,0:T(8,128)(2,1)}, bf16[64,192]{1,0:T(8,128)(2,1)}, bf16[16,384]{1,0:T(8,128)(2,1)}) custom-call(bf16[4,384,128]{2,1,0:T(8,128)(2,1)} %exchange.1.held, bf16[720,720]{1,0:T(8,128)(2,1)} %weight_ref.1, f32[720,1]{1,0:T(8,128)} %broadcast_in_dim.13.bias_ref), custom_call_target="tpu_custom_call" | custom-call | tf_op jit(solution)/shard_map/join/pallas_call | solution.py:533
Async XLA Ops:
  9.1 27.5 %copy-start.1 = (f32[720]{0:T(1024)S(1)}, f32[720]{0:T(1024)}, u32[]{:S(2)}) copy-start(f32[720]{0:T(1024)} %param.13) | copy-start | bytes 8644
